TPU v7x, 32 devices: a whole 2x2x4 slice. The times are simulated.
32 devices in a mesh: rows: 8 (over z, y), rep: 4 (over x, core).
Axes of the slice: x: 2, y: 2, z: 4, core: 2. Of those that a mesh axis runs over, the one named last changes fastest.
Arguments:
- tables: bfloat16 [16384, 128], P('rows'), may hold values from -0.5 to 0.5
- indices: int32 [512, 8, 8], P(('rows', 'rep')), may hold values from 0 to 2047
- bag_lengths: int32 [512, 8], P(('rows', 'rep')), may hold values from 1 to 8
- dense: bfloat16 [512, 13], P(('rows', 'rep')), may hold values from -6 to 6
- bottom_first: bfloat16 [13, 512], replicated, may hold values from -1.75 to 1.75
- bottom_second: bfloat16 [512, 256], replicated, may hold values from -0.375 to 0.375
- bottom_third: bfloat16 [256, 128], replicated, may hold values from -0.5 to 0.5
- top_first: bfloat16 [164, 1024], P(None, 'rep'), may hold values from -0.5 to 0.5
- top_second: bfloat16 [1024, 1024], P(None, 'rep'), may hold values from -0.25 to 0.25
- top_third: bfloat16 [1024, 512], P(None, 'rep'), may hold values from -0.25 to 0.25
- top_fourth: bfloat16 [512, 256], P(None, 'rep'), may hold values from -0.375 to 0.375
- top_last: bfloat16 [256], replicated, may hold values from -0.5 to 0.5
Outputs:
- logit: float32 [512], P(('rows', 'rep'))
Inputs may be any that keep to these rules, and one draw needn't show every extreme that they name: `indices`: each entry is a row number within its own table; entries at positions of a bag at or past its length are ignored.
All inputs are finite; a program needn't handle non-finite values.
Results may differ from a plain program's by a relative error of at most 0.0076.
Values may be sent and summed in bfloat16 or wider, within the bound.
A program may use at most 64 MiB of HBM per device.

v0:
```python
import functools

import jax
import jax.numpy as jnp
from jax import lax
from jax.experimental import pallas as pl
from jax.experimental.pallas import tpu as pltpu
from jax.sharding import PartitionSpec as P

TAB = 8
HOT = 8
LANES = 128
MESH = pl.DeviceIdType.MESH
BF16 = jnp.bfloat16
F32 = jnp.float32


def flip(k, offset):
    bit = 1
    while bit <= offset:
        if offset & bit:
            k = k + bit - 2 * bit * ((k // bit) % 2)
        bit *= 2
    return k


def dot(a, b):
    return jnp.dot(a, b, preferred_element_type=F32)


def dot_t(a, b):
    return lax.dot_general(a, b, (((1,), (1,)), ((), ())), preferred_element_type=F32)


def run_half(lookup, base, count):
    if count == 4:
        lookup(base)
    else:
        pl.loop(0, count // 4)(lambda g: lookup(base + 4 * g))


def relu_round(x):
    return jnp.maximum(x, 0.0).astype(BF16)


def kernel(
    D,
    R,
    tables,
    indices_h,
    lengths_h,
    dense_h,
    bottom_first_h,
    bottom_second_h,
    bottom_third_h,
    top_first,
    top_second,
    top_third,
    top_fourth,
    top_last_h,
    out,
    indices,
    bag_lengths,
    dense,
    bottom_first,
    bottom_second,
    bottom_third,
    top_last,
    table_v,
    w1,
    w2,
    w3,
    w4,
    out_idx,
    recv_idx,
    counts,
    part,
    recv_pool,
    recv_top,
    act1,
    act2,
    recv_act2,
    local_sem,
    e1_send,
    e1_recv,
    e2_send,
    e2_recv,
    e3_send,
    e3_recv,
    e4_send,
    e4_recv,
    w_send,
    w_recv,
):
    B = indices.shape[2]
    rows = tables.shape[0]
    per_table = D // TAB
    me = lax.axis_index("rows")
    k = lax.axis_index("rep")

    barrier = pltpu.get_barrier_semaphore()
    for d in range(1, D):
        pl.semaphore_signal(
            barrier, inc=1, device_id=(lax.rem(me + d, D), k), device_id_type=MESH
        )
    for o in range(1, R):
        pl.semaphore_signal(barrier, inc=1, device_id=(me, flip(k, o)), device_id_type=MESH)

    small = [
        pltpu.make_async_copy(indices_h, indices, local_sem.at[5]),
        pltpu.make_async_copy(lengths_h, bag_lengths, local_sem.at[6]),
        pltpu.make_async_copy(dense_h, dense, local_sem.at[7]),
        pltpu.make_async_copy(bottom_first_h, bottom_first, local_sem.at[8]),
        pltpu.make_async_copy(bottom_second_h, bottom_second, local_sem.at[9]),
        pltpu.make_async_copy(bottom_third_h, bottom_third, local_sem.at[10]),
        pltpu.make_async_copy(top_last_h, top_last, local_sem.at[11]),
    ]
    local = [
        pltpu.make_async_copy(tables, table_v, local_sem.at[0]),
        pltpu.make_async_copy(top_first, w1.at[k], local_sem.at[1]),
        pltpu.make_async_copy(top_second, w2, local_sem.at[2]),
        pltpu.make_async_copy(top_third, w3.at[k], local_sem.at[3]),
        pltpu.make_async_copy(top_fourth, w4.at[k], local_sem.at[4]),
    ]
    for copy in small + local:
        copy.start()

    small[0].wait()
    small[1].wait()
    lens = bag_lengths[...]
    out_idx[...] = jnp.concatenate(
        [jnp.where(lens > s, indices[:, s, :], -1) for s in range(HOT)], axis=1
    ).reshape(TAB, 1, B * HOT)

    pl.semaphore_wait(barrier, D - 1 + R - 1)

    sends = []

    def send(src, dst, ssem, rsem, device):
        copy = pltpu.make_async_remote_copy(
            src_ref=src,
            dst_ref=dst,
            send_sem=ssem,
            recv_sem=rsem,
            device_id=device,
            device_id_type=MESH,
        )
        copy.start()
        sends.append(copy)
        return copy

    first = {}
    for d in reversed(range(1, D)):
        peer = flip(me, d)
        first[d] = send(
            out_idx.at[peer // per_table], recv_idx.at[me], e1_send.at[d], e1_recv.at[d], (peer, k)
        )
    recv_idx[me] = out_idx[me // per_table]

    mine = (top_first, top_third, top_fourth)
    whole = (w1, w3, w4)
    arriving = {}
    stages = []
    held = [0]
    bit = R // 2
    while bit:
        stages.append([(bit, h) for h in held])
        held = held + [h ^ bit for h in held]
        bit //= 2

    def weight_send(array, bit, h):
        block = flip(k, h)
        src = mine[array] if h == 0 else whole[array].at[block]
        arriving[array, h ^ bit] = send(
            src,
            whole[array].at[block],
            w_send.at[array * R + (h ^ bit)],
            w_recv.at[array * R + (h ^ bit)],
            (me, flip(k, bit)),
        )

    for array in range(3):
        for stage in stages:
            for bit, h in stage:
                if h == 0:
                    weight_send(array, bit, h)

    got = set()

    def weight_forward(array):
        for stage in stages:
            for bit, h in stage:
                if h != 0:
                    if (array, h) not in got:
                        arriving[array, h].wait_recv()
                        got.add((array, h))
                    weight_send(array, bit, h)

    def weight_finish(array):
        for o in range(1, R):
            if (array, o) not in got:
                arriving[array, o].wait_recv()
                got.add((array, o))

    for copy in small[2:]:
        copy.wait()
    lower = relu_round(dot(dense[...], bottom_first[...]))
    middle = relu_round(dot(lower, bottom_second[...]))
    bottom_out = jnp.maximum(dot(middle, bottom_third[...]), 0.0)

    local[0].wait()

    offset = (me % per_table) * rows
    lanes = lax.broadcasted_iota(jnp.int32, (16, LANES), 1).astype(F32).astype(BF16)
    one, zero = jnp.ones((16, LANES), BF16), jnp.zeros((16, LANES), BF16)
    half = B // 2

    def lookup(base):
        rows4 = recv_idx[pl.ds(base, 4)].reshape(4, B * HOT) - offset
        wanted = jnp.concatenate([rows4, pltpu.roll(rows4, B * HOT - half, 1)], axis=0)
        blocks = rows // LANES
        for pair in range(half // 2):
            totals = [jnp.zeros((16, LANES), BF16)] * blocks
            for s in range(HOT):
                j = B * s + 2 * pair
                entry = jnp.concatenate([wanted[:, j : j + 1], wanted[:, j + 1 : j + 2]], axis=0)
                entry = jnp.broadcast_to(entry, (16, LANES))
                high_part = (entry >> 7).astype(F32).astype(BF16)
                low_part = (entry & (LANES - 1)).astype(F32).astype(BF16)
                hit = jnp.where(low_part == lanes, one, zero)
                for n in range(blocks):
                    here = jnp.where(high_part == jnp.asarray(n, BF16), hit, zero)
                    totals[n] = totals[n] + here
            for n in range(blocks):
                counts[16 * pair : 16 * pair + 16, n * LANES : (n + 1) * LANES] = totals[n]
        partial = dot(counts[...], table_v[...])
        for b in range(half):
            part[pl.ds(base, 4), b, :] = partial[8 * b : 8 * b + 4, :]
            part[pl.ds(base, 4), b + half, :] = partial[8 * b + 4 : 8 * b + 8, :]

    second = []

    def second_send(d):
        peer = flip(me, d)
        second.append(
            send(part.at[peer], recv_pool.at[me], e2_send.at[d], e2_recv.at[d], (peer, k))
        )

    low, high = D // 2, D
    for d in range(1, low):
        first[d].wait_recv()
    run_half(lookup, me // low * low, low)
    for d in range(1, low):
        second_send(d)
    for d in range(low, high):
        first[d].wait_recv()
    run_half(lookup, (1 - me // low) * low, low)
    for d in range(low, high):
        second_send(d)
    recv_pool[me] = part[me]
    weight_forward(0)
    for copy in second:
        copy.wait_recv()

    features = [bottom_out]
    for t in range(TAB):
        pooled = recv_pool[t * per_table]
        for i in range(1, per_table):
            pooled = pooled + recv_pool[t * per_table + i]
        features.append(pooled)
    E = bottom_out.shape[1]
    lane = lax.broadcasted_iota(jnp.int32, (B, E), 1)
    dots = jnp.zeros((B, E), F32)
    p = 0
    for i in range(TAB + 1):
        for j in range(i + 1, TAB + 1):
            value = jnp.sum(features[i] * features[j], axis=1, keepdims=True)
            dots = jnp.where(lane == p, value, dots)
            p += 1
    recv_top[k] = jnp.concatenate([bottom_out, dots], axis=1).astype(BF16)

    third = [
        send(recv_top.at[k], recv_top.at[k], e3_send.at[o], e3_recv.at[o], (me, flip(k, o)))
        for o in range(1, R)
    ]
    weight_finish(0)
    weight_forward(1)
    weight_forward(2)
    for copy in local[1:]:
        copy.wait()
    for copy in third:
        copy.wait_recv()

    top_in = recv_top[...].reshape(R * B, 2 * E)
    n1 = w1.shape[2]
    for n in range(R):
        act1[:, n * n1 : (n + 1) * n1] = relu_round(
            dot(top_in[:, :E], w1[n, :E, :]) + dot(top_in[:, E : E + p], w1[n, E:, :])
        )
    act2[...] = relu_round(dot(act1[...], w2[...])).reshape(act2.shape)

    fourth = [
        send(
            act2.at[flip(k, o)], recv_act2.at[k], e4_send.at[o], e4_recv.at[o], (me, flip(k, o))
        )
        for o in range(1, R)
    ]
    recv_act2[k] = act2[k]
    weight_finish(1)
    weight_finish(2)
    for copy in fourth:
        copy.wait_recv()

    third_in = jnp.concatenate([recv_act2[n] for n in range(R)], axis=1)
    fourth_in = jnp.concatenate([relu_round(dot(third_in, w3[n])) for n in range(R)], axis=1)
    last_in = jnp.concatenate([relu_round(dot_t(fourth_in, w4[n])) for n in range(R)], axis=1)
    out[...] = dot_t(top_last[...].reshape(1, -1), last_in).reshape(B)
    for copy in sends:
        copy.wait_send()


def body(*args):
    (tables, indices, bag_lengths, dense, b1, b2, b3, t1, t2, t3, t4, last) = args
    D = lax.axis_size("rows")
    R = lax.axis_size("rep")
    B = indices.shape[0]
    indices = jnp.transpose(indices, (1, 2, 0))
    bag_lengths = jnp.transpose(bag_lengths)
    t4 = jnp.transpose(t4)
    E = tables.shape[1]
    vmem = pl.BlockSpec(memory_space=pltpu.VMEM)
    hbm = pl.BlockSpec(memory_space=pl.ANY)
    dma = pltpu.SemaphoreType.DMA
    result = pl.pallas_call(
        functools.partial(kernel, D, R),
        out_shape=jax.ShapeDtypeStruct((B,), F32),
        in_specs=[hbm] * 12,
        out_specs=vmem,
        scratch_shapes=[
            pltpu.VMEM(indices.shape, jnp.int32),
            pltpu.VMEM(bag_lengths.shape, jnp.int32),
            pltpu.VMEM(dense.shape, BF16),
            pltpu.VMEM(b1.shape, BF16),
            pltpu.VMEM(b2.shape, BF16),
            pltpu.VMEM(b3.shape, BF16),
            pltpu.VMEM(last.shape, BF16),
            pltpu.VMEM(tables.shape, BF16),
            pltpu.VMEM((R,) + t1.shape, BF16),
            pltpu.VMEM(t2.shape, BF16),
            pltpu.VMEM((R,) + t3.shape, BF16),
            pltpu.VMEM((R,) + t4.shape, BF16),
            pltpu.VMEM((TAB, 1, B * HOT), jnp.int32),
            pltpu.VMEM((D, 1, B * HOT), jnp.int32),
            pltpu.VMEM((4 * B, tables.shape[0]), BF16),
            pltpu.VMEM((D, B, E), F32),
            pltpu.VMEM((D, B, E), F32),
            pltpu.VMEM((R, B, 2 * E), BF16),
            pltpu.VMEM((R * B, R * t1.shape[1]), BF16),
            pltpu.VMEM((R, B, t2.shape[1]), BF16),
            pltpu.VMEM((R, B, t2.shape[1]), BF16),
            dma((12,)),
            dma((D,)),
            dma((D,)),
            dma((D,)),
            dma((D,)),
            dma((R,)),
            dma((R,)),
            dma((R,)),
            dma((R,)),
            dma((3 * R,)),
            dma((3 * R,)),
        ],
        compiler_params=pltpu.CompilerParams(collective_id=0, has_side_effects=True),
    )(tables, indices, bag_lengths, dense, b1, b2, b3, t1, t2, t3, t4, last)
    return result


def solution(mesh):
    placed = (
        P("rows", None),
        P(("rows", "rep"), None, None),
        P(("rows", "rep"), None),
        P(("rows", "rep"), None),
        P(),
        P(),
        P(),
        P(None, "rep"),
        P(None, "rep"),
        P(None, "rep"),
        P(None, "rep"),
        P(),
    )
    return jax.shard_map(
        body, mesh=mesh, in_specs=placed, out_specs=P(("rows", "rep")), check_vma=False
    )
```

profile of v0, /device:TPU:0, one launch (start us, length us, event | category | flops | bytes accessed | tf_op | source)
XLA Modules:
  0.0 23.9 jit_solution(6477466835330951116)
XLA Ops:
  0.0 22.7 %shard_map.118 = f32[16]{0:T(128)} custom-call(bf16[2048,128]{1,0:T(8,128)(2,1)} %tables.1, s32[8,8,16]{2,1,0:T(8,128)} %bitcast.4, s32[8,16]{1,0:T(8,128)} %bitcast.5, bf16[16,13]{1,0:T(8,128)(2,1)} %dense_h.1, bf16[13,512]{1,0:T(8,128)(2,1)} %bottom_first_h.1, bf16[512,256]{1,0:T(8,128)(2,1)} %bottom_second_h.1, bf16[256,128]{1,0:T(8,128)(2,1)} %bottom_third_h.1, ...), custom_call_target="tpu_custom_call" | custom-call | tf_op jit(solution)/shard_map/pallas_call | solution.py:334
  22.7 1.2 %copy.14 = f32[16]{0:T(128)} copy(f32[16]{0:T(128)} %shard_map.118) | data formatting | bytes 128
where the time goes:
time: 24.1 us; the launch traced here: 23.9 us
  Pallas kernels  22.7 us (94%)
  local copies, waits for them, and re-layouts  1.19 us (5%)
    pallas_call x1, Pallas kernels, body(): pl.pallas_call(functools.partial(kernel, D, R), out_shape=jax.ShapeDtypeS...  22.7 us
    unnamed x1, local copies, waits for them, and re-layouts  1.19 us

commit v1 on v0

--- a/solution.py
+++ b/solution.py
@@ -333,7 +333,7 @@
     dma = pltpu.SemaphoreType.DMA
     result = pl.pallas_call(
         functools.partial(kernel, D, R),
-        out_shape=jax.ShapeDtypeStruct((B,), F32),
+        out_shape=pltpu.VMEM((B,), F32),
         in_specs=[hbm] * 12,
         out_specs=vmem,
         scratch_shapes=[

time: 24.1 us -> 22.8 us (0.946)
  local copies, waits for them, and re-layouts: 1.19 us -> 0.51 us
  Pallas kernels: 22.7 us -> 22.1 us
    unnamed x1, local copies, waits for them, and re-layouts: 1.19 us -> 0.51 us
    pallas_call x1, Pallas kernels: 22.7 us -> 22.1 us  [body(): pl.pallas_call(functools.partial(kernel, D, R), out_shape=pltpu.VMEM((B,)...]
where the time goes in v1:
time: 22.8 us; the launch traced here: 22.7 us
  Pallas kernels  22.1 us (97%)
  local copies, waits for them, and re-layouts  0.51 us (2%)
    pallas_call x1, Pallas kernels, body(): pl.pallas_call(functools.partial(kernel, D, R), out_shape=pltpu.VMEM((B,)...  22.1 us
    unnamed x1, local copies, waits for them, and re-layouts  0.51 us

profile of v1, /device:TPU:0, one launch (start us, length us, event | category | flops | bytes accessed | tf_op | source)
XLA Modules:
  0.0 22.7 jit_solution(7940561922155084316)
XLA Ops:
  0.0 22.1 %shard_map.118 = f32[16]{0:T(128)S(1)} custom-call(bf16[2048,128]{1,0:T(8,128)(2,1)} %tables.1, s32[8,8,16]{2,1,0:T(8,128)} %bitcast.4, s32[8,16]{1,0:T(8,128)} %bitcast.5, bf16[16,13]{1,0:T(8,128)(2,1)} %dense_h.1, bf16[13,512]{1,0:T(8,128)(2,1)} %bottom_first_h.1, bf16[512,256]{1,0:T(8,128)(2,1)} %bottom_second_h.1, bf16[256,128]{1,0:T(8,128)(2,1)} %bottom_third_h.1, ...), custom_call_target="tpu_custom_call" | custom-call | tf_op jit(solution)/shard_map/pallas_call | solution.py:334
  22.2 0.5 %copy.14 = f32[16]{0:T(128)} copy(f32[16]{0:T(128)S(1)} %shard_map.118) | data formatting | bytes 128

commit v2 on v1

v2 whole, which is shorter than its diff:
```python
import functools

import jax
import jax.numpy as jnp
from jax import lax
from jax.experimental import pallas as pl
from jax.experimental.pallas import tpu as pltpu
from jax.sharding import PartitionSpec as P

TAB = 8
HOT = 8
LANES = 128
PACK = 16
SHIFT = 4
CHUNK = 256
SPAN = 65536
(S_IDX, R_IDX, S_DENSE, R_DENSE, S_W1, R_W1, S_W2, R_W2) = range(7, 15)
(S_E1, R_E1A, R_E1B, S_E2, R_E2, S_E3, R_E3, S_E4, R_E4) = range(15, 24)
S_OWN, S_FORWARD, R_DOWN, R_ACROSS = 24, 26, 28, 30
MESH = pl.DeviceIdType.MESH
BF16 = jnp.bfloat16
F32 = jnp.float32


def flip(k, offset):
    bit = 1
    while bit <= offset:
        if offset & bit:
            k = k + bit - 2 * bit * ((k // bit) % 2)
        bit *= 2
    return k


def dot(a, b):
    return jnp.dot(a, b, preferred_element_type=F32)


def dot_t(a, b):
    return lax.dot_general(a, b, (((1,), (1,)), ((), ())), preferred_element_type=F32)


def relu_round(x):
    return jnp.maximum(x, 0.0).astype(BF16)


def kernel(
    D,
    R,
    tables,
    indices_h,
    lengths_h,
    dense_h,
    bottom_first_h,
    bottom_second_h,
    bottom_third_h,
    top_first,
    top_second,
    top_third,
    top_fourth,
    top_last_h,
    out,
    indices,
    bag_lengths,
    dense,
    bottom_first,
    bottom_second,
    bottom_third,
    top_last,
    table_v,
    table_t,
    w1,
    w2,
    w3,
    w4,
    own_idx,
    pair_idx,
    out_idx,
    recv_idx,
    part,
    recv_pool,
    recv_top,
    act1,
    act2,
    recv_act2,
    go,
    sem,
):
    B = indices.shape[2]
    rows, E = tables.shape
    X = R // 2
    group = LANES // (2 * B)
    per_table = D // TAB
    me = lax.axis_index("rows")
    k = lax.axis_index("rep")
    core = k % 2
    x = k // 2
    mate = flip(k, 1)
    low, high = D // 2, D

    barrier = pltpu.get_barrier_semaphore()

    def greet(device):
        pl.semaphore_signal(barrier, inc=1, device_id=device, device_id_type=MESH)

    def local(src, dst, i):
        copy = pltpu.make_async_copy(src, dst, sem.at[i])
        copy.start()
        return copy

    def remote(src, dst, ssem, rsem, device):
        return pltpu.make_async_remote_copy(
            src_ref=src,
            dst_ref=dst,
            send_sem=sem.at[ssem],
            recv_sem=sem.at[rsem],
            device_id=device,
            device_id_type=MESH,
        )

    def send(src, dst, ssem, rsem, device):
        remote(src, dst, ssem, rsem, device).start()

    def arrive(dst, rsem):
        remote(dst, dst, rsem, rsem, (me, mate)).wait_recv()

    def sent(src, ssem):
        remote(src, src, ssem, ssem, (me, mate)).wait_send()

    def sent_blocks(stack, count, ssem):
        while count:
            now = min(count, stack.shape[0])
            sent(stack.at[pl.ds(0, now)], ssem)
            count -= now

    def own_tile():
        lens = bag_lengths[...].reshape(TAB, 1, B)
        slot = lax.broadcasted_iota(jnp.int32, (TAB, HOT, B), 1)
        own_idx[...] = jnp.full(own_idx.shape, -1, jnp.int32)
        own_idx[:, :, :B] = jnp.where(slot < lens, indices[...], -1)
        place = B * (2 * (me % group) + core)
        slot = lax.broadcasted_iota(jnp.int32, (HOT, LANES), 0)
        tiles = []
        for t in range(TAB):
            entry = own_idx[t]
            many = jnp.ones(entry.shape, jnp.int32)
            again = entry < 0
            for r in range(1, HOT):
                other = pltpu.roll(entry, r, 0)
                same = entry == other
                many = many + jnp.where(same, 1, 0)
                again = jnp.logical_or(again, jnp.logical_and(same, slot >= r))
            entry = jnp.where(again, -1, entry + many * SPAN)
            tiles.append(pltpu.roll(entry, place, 1))
        return jnp.stack(tiles)

    halves = (top_third, top_fourth)
    whole = (w3, w4)

    def finish():
        third_in = jnp.concatenate([recv_act2[n] for n in range(X)], axis=1)
        fourth_in = jnp.concatenate([relu_round(dot(third_in, w3[n])) for n in range(R)], axis=1)
        last_in = jnp.concatenate([relu_round(dot_t(fourth_in, w4[n])) for n in range(R)], axis=1)
        out[...] = dot_t(top_last[...].reshape(1, -1), last_in).reshape(B)

    greet((me, mate))
    for o in range(1, X):
        greet((me, 2 * flip(x, o) + 1))
    get_idx = local(indices_h, indices, 0)
    get_len = local(lengths_h, bag_lengths, 1)

    @pl.when(core == 0)
    def follower():
        later = [
            local(top_third, w3.at[k], 2),
            local(top_fourth, w4.at[k], 3),
            local(top_last_h, top_last, 4),
        ]
        get_idx.wait()
        get_len.wait()
        pair_idx[...] = own_tile()
        pl.semaphore_wait(barrier, 1)
        up = (me, mate)
        send(pair_idx, pair_idx, S_IDX, R_IDX, up)
        send(dense_h, dense.at[0], S_DENSE, R_DENSE, up)
        send(top_first, w1.at[k], S_W1, R_W1, up)
        send(top_second, w2.at[0], S_W2, R_W2, up)
        for a in range(2):
            send(halves[a], whole[a].at[k], S_OWN + a, R_DOWN + a, up)
        pl.semaphore_wait(go, 1)

        def over(a, src, block, ssem, h):
            for o in range(1, X):
                send(
                    src,
                    whole[a].at[block],
                    ssem,
                    R_ACROSS + a * R + 2 * o + h,
                    (me, flip(k, 2 * o)),
                )

        for o in range(1, X):
            send(top_first, w1.at[k], S_W1, R_W1, (me, flip(k, 2 * o + 1)))
        for a in range(2):
            over(a, halves[a], k, S_OWN + a, 0)
        for a in range(2):
            arrive(whole[a].at[mate], R_ACROSS + a * R)
            over(a, whole[a].at[mate], mate, S_FORWARD + a, 1)
        for h in range(2):
            for a in range(2):
                for o in range(1, X):
                    block = whole[a].at[flip(k, 2 * o + h)]
                    arrive(block, R_ACROSS + a * R + 2 * o + h)
                    send(block, block, S_FORWARD + a, R_DOWN + a, up)
        for copy in later:
            copy.wait()
        arrive(recv_act2, R_E4)
        finish()
        sent(pair_idx, S_IDX)
        sent(dense.at[0], S_DENSE)
        sent(w2.at[0], S_W2)
        sent_blocks(w1, X, S_W1)
        for a in range(2):
            sent_blocks(whole[a], X, S_OWN + a)
            sent_blocks(whole[a], 3 * (X - 1), S_FORWARD + a)

    @pl.when(core == 1)
    def leader():
        for d in range(1, D):
            greet((flip(me, d), k))
        get_dense = local(dense_h, dense.at[1], 2)
        get_bottom = [
            local(bottom_first_h, bottom_first, 3),
            local(bottom_second_h, bottom_second, 4),
            local(bottom_third_h, bottom_third, 5),
        ]
        get_table = local(tables, table_v, 6)
        get_idx.wait()
        get_len.wait()
        later = [local(top_second, w2.at[1], 0), local(top_first, w1.at[k], 1)]
        mine = own_tile()
        pl.semaphore_wait(barrier, D - 1 + 1 + 2 * (X - 1))
        arrive(pair_idx, R_IDX)
        out_idx[...] = jnp.maximum(mine, pair_idx[...])

        for d in reversed(range(1, D)):
            peer = flip(me, d)
            send(
                out_idx.at[peer // per_table],
                recv_idx.at[me],
                S_E1,
                R_E1A if d < low else R_E1B,
                (peer, k),
            )
        pl.semaphore_signal(go, inc=1, device_id=(me, mate), device_id_type=MESH)
        recv_idx[me] = out_idx[me // per_table]
        for o in range(1, X):
            send(top_first, w1.at[k], S_W1, R_W1, (me, flip(k, 2 * o)))
        for a in range(2):
            send(halves[a], whole[a].at[k], S_OWN + a, R_ACROSS + a * R, (me, mate))

        get_table.wait()
        table_t[...] = table_v[...].T

        get_dense.wait()
        for copy in get_bottom:
            copy.wait()
        later += [
            local(top_third, w3.at[k], 2),
            local(top_fourth, w4.at[k], 3),
            local(top_last_h, top_last, 4),
        ]
        arrive(dense.at[0], R_DENSE)
        lower = relu_round(dot(dense[...].reshape(2 * B, -1), bottom_first[...]))
        middle = relu_round(dot(lower, bottom_second[...]))
        bottom_out = jnp.maximum(dot(middle, bottom_third[...]), 0.0)

        offset = (me % per_table) * rows
        sub = lax.broadcasted_iota(jnp.int32, (PACK, LANES), 0)
        zero = jnp.zeros((PACK, LANES), BF16)

        def lookup(g):
            base = group * g
            entry = recv_idx[base]
            for i in range(1, group):
                entry = jnp.maximum(entry, recv_idx[base + i])
            codes, counts = [], []
            for s in range(HOT):
                row = jnp.broadcast_to(entry[s : s + 1, :], (PACK, LANES))
                spot = (row & (SPAN - 1)) - offset
                hit = jnp.logical_and((spot & (PACK - 1)) == sub, row >= 0)
                codes.append(jnp.where(hit, spot >> SHIFT, -1).astype(F32).astype(BF16))
                counts.append((row // SPAN).astype(F32).astype(BF16))
            partial = jnp.zeros((E, LANES), F32)
            for c in range(rows // CHUNK):
                chunk = []
                for n in range(c * CHUNK // PACK, (c + 1) * CHUNK // PACK):
                    total = zero
                    for code, count in zip(codes, counts):
                        total = jnp.where(code == jnp.asarray(n, BF16), count, total)
                    chunk.append(total)
                partial = partial + dot(
                    table_t[:, c * CHUNK : (c + 1) * CHUNK], jnp.concatenate(chunk, axis=0)
                )
            part[pl.ds(base, group)] = partial.T.reshape(group, 2 * B, E)

        def run(base, count):
            if count == group:
                lookup(base // group)
            else:
                pl.loop(0, count // group)(lambda g: lookup(base // group + g))

        def second_send(d):
            peer = flip(me, d)
            send(part.at[peer], recv_pool.at[me], S_E2, R_E2, (peer, k))

        arrive(recv_idx.at[pl.ds(0, low - 1)], R_E1A)
        run(me // low * low, low)
        for d in range(1, low):
            second_send(d)
        arrive(recv_idx.at[pl.ds(0, low)], R_E1B)
        run((1 - me // low) * low, low)
        for d in range(low, high):
            second_send(d)
        recv_pool[me] = part[me]
        arrive(recv_pool.at[pl.ds(0, D - 1)], R_E2)

        features = [bottom_out]
        for t in range(TAB):
            pooled = recv_pool[t * per_table]
            for i in range(1, per_table):
                pooled = pooled + recv_pool[t * per_table + i]
            features.append(pooled)
        lane = lax.broadcasted_iota(jnp.int32, (2 * B, E), 1)
        dots = jnp.zeros((2 * B, E), F32)
        p = 0
        for i in range(TAB + 1):
            for j in range(i + 1, TAB + 1):
                value = jnp.sum(features[i] * features[j], axis=1, keepdims=True)
                dots = jnp.where(lane == p, value, dots)
                p += 1
        recv_top[x] = jnp.concatenate([bottom_out, dots], axis=1).astype(BF16)

        for o in range(1, X):
            send(recv_top.at[x], recv_top.at[x], S_E3, R_E3, (me, flip(k, 2 * o)))
        for copy in later:
            copy.wait()
        arrive(w1.at[pl.ds(0, R - 1)], R_W1)
        arrive(w2.at[0], R_W2)
        if X > 1:
            arrive(recv_top.at[pl.ds(0, X - 1)], R_E3)

        top_in = recv_top[...].reshape(R * B, 2 * E)
        n1, n2 = w1.shape[2], w2.shape[2]
        for n in range(R):
            act1[:, n * n1 : (n + 1) * n1] = relu_round(
                dot(top_in[:, :E], w1[n, :E, :]) + dot(top_in[:, E : E + p], w1[n, E:, :])
            )
        for j in range(2):
            act2[:, :, j * n2 : (j + 1) * n2] = relu_round(dot(act1[...], w2[j])).reshape(
                R, B, n2
            )
        for o in range(1, X):
            for h in range(2):
                to = flip(k, 2 * o + h)
                send(act2.at[to], recv_act2.at[x], S_E4, R_E4, (me, to))
        send(act2.at[mate], recv_act2.at[x], S_E4, R_E4, (me, mate))
        recv_act2[x] = act2[k]
        for a in range(2):
            arrive(whole[a].at[pl.ds(0, R - 1)], R_DOWN + a)
        if X > 1:
            arrive(recv_act2.at[pl.ds(0, X - 1)], R_E4)
        finish()
        sent(recv_idx.at[pl.ds(0, D - 1)], S_E1)
        sent(part.at[pl.ds(0, D - 1)], S_E2)
        for a in range(2):
            sent(whole[a].at[k], S_OWN + a)
        sent(act2.at[pl.ds(0, R - 1)], S_E4)
        if X > 1:
            sent_blocks(w1, X - 1, S_W1)
            sent(recv_top.at[pl.ds(0, X - 1)], S_E3)


def body(*args):
    (tables, indices, bag_lengths, dense, b1, b2, b3, t1, t2, t3, t4, last) = args
    D = lax.axis_size("rows")
    R = lax.axis_size("rep")
    B = indices.shape[0]
    indices = jnp.transpose(indices, (1, 2, 0))
    bag_lengths = jnp.transpose(bag_lengths)
    t4 = jnp.transpose(t4)
    rows, E = tables.shape
    X = R // 2
    hbm = pl.BlockSpec(memory_space=pl.ANY)
    tile = pltpu.VMEM((TAB, HOT, LANES), jnp.int32)
    result = pl.pallas_call(
        functools.partial(kernel, D, R),
        out_shape=pltpu.VMEM((B,), F32),
        in_specs=[hbm] * 12,
        out_specs=pl.BlockSpec(memory_space=pltpu.VMEM),
        scratch_shapes=[
            pltpu.VMEM(indices.shape, jnp.int32),
            pltpu.VMEM(bag_lengths.shape, jnp.int32),
            pltpu.VMEM((2,) + dense.shape, BF16),
            pltpu.VMEM(b1.shape, BF16),
            pltpu.VMEM(b2.shape, BF16),
            pltpu.VMEM(b3.shape, BF16),
            pltpu.VMEM(last.shape, BF16),
            pltpu.VMEM((rows, E), BF16),
            pltpu.VMEM((E, rows), BF16),
            pltpu.VMEM((R,) + t1.shape, BF16),
            pltpu.VMEM((2,) + t2.shape, BF16),
            pltpu.VMEM((R,) + t3.shape, BF16),
            pltpu.VMEM((R,) + t4.shape, BF16),
            tile,
            tile,
            tile,
            pltpu.VMEM((D, HOT, LANES), jnp.int32),
            pltpu.VMEM((D, 2 * B, E), F32),
            pltpu.VMEM((D, 2 * B, E), F32),
            pltpu.VMEM((X, 2 * B, 2 * E), BF16),
            pltpu.VMEM((R * B, R * t1.shape[1]), BF16),
            pltpu.VMEM((R, B, 2 * t2.shape[1]), BF16),
            pltpu.VMEM((X, B, 2 * t2.shape[1]), BF16),
            pltpu.SemaphoreType.REGULAR,
            pltpu.SemaphoreType.DMA((R_ACROSS + 2 * R,)),
        ],
        compiler_params=pltpu.CompilerParams(collective_id=0, has_side_effects=True),
    )(tables, indices, bag_lengths, dense, b1, b2, b3, t1, t2, t3, t4, last)
    return result


def solution(mesh):
    placed = (
        P("rows", None),
        P(("rows", "rep"), None, None),
        P(("rows", "rep"), None),
        P(("rows", "rep"), None),
        P(),
        P(),
        P(),
        P(None, "rep"),
        P(None, "rep"),
        P(None, "rep"),
        P(None, "rep"),
        P(),
    )
    return jax.shard_map(
        body, mesh=mesh, in_specs=placed, out_specs=P(("rows", "rep")), check_vma=False
    )
```

time: 22.8 us -> 19.8 us (0.87)
  Pallas kernels: 22.1 us -> 19.1 us
    pallas_call x1, Pallas kernels: 22.1 us -> 19.1 us  [body(): pl.pallas_call(functools.partial(kernel, D, R), out_shape=pltpu.VMEM((B,)...]
where the time goes in v2:
time: 19.8 us; the launch traced here: 19.7 us
  Pallas kernels  19.1 us (96%)
  local copies, waits for them, and re-layouts  0.51 us (3%)
    pallas_call x1, Pallas kernels, body(): pl.pallas_call(functools.partial(kernel, D, R), out_shape=pltpu.VMEM((B,)...  19.1 us
    unnamed x1, local copies, waits for them, and re-layouts  0.51 us

profile of v2, /device:TPU:0, one launch (start us, length us, event | category | flops | bytes accessed | tf_op | source)
XLA Modules:
  0.0 19.7 jit_solution(2544088387985357132)
XLA Ops:
  0.0 19.1 %shard_map.118 = f32[16]{0:T(128)S(1)} custom-call(bf16[2048,128]{1,0:T(8,128)(2,1)} %tables.1, s32[8,8,16]{2,1,0:T(8,128)} %bitcast.4, s32[8,16]{1,0:T(8,128)} %bitcast.5, bf16[16,13]{1,0:T(8,128)(2,1)} %dense_h.1, bf16[13,512]{1,0:T(8,128)(2,1)} %bottom_first_h.1, bf16[512,256]{1,0:T(8,128)(2,1)} %bottom_second_h.1, bf16[256,128]{1,0:T(8,128)(2,1)} %bottom_third_h.1, ...), custom_call_target="tpu_custom_call" | custom-call | tf_op jit(solution)/shard_map/pallas_call | solution.py:395
  19.2 0.5 %copy.14 = f32[16]{0:T(128)} copy(f32[16]{0:T(128)S(1)} %shard_map.118) | data formatting | bytes 128

commit v3 on v2

v3 whole, which is shorter than its diff:
```python
import functools

import jax
import jax.numpy as jnp
from jax import lax
from jax.experimental import pallas as pl
from jax.experimental.pallas import tpu as pltpu
from jax.sharding import PartitionSpec as P

TAB = 8
HOT = 8
LANES = 128
PACK = 16
SHIFT = 4
CHUNK = 256
EARLY = 4
SPAN = 65536
S_DENSE, S_W1, S_W3, S_OWN, S_E4, R_IDX, R_DENSE, R_W1, R_W2, R_W3, R_E4, R_DOWN = range(7, 19)
S_E1, S_E2, S_E3, R_E1A, R_E1B, R_E2, R_E2X, R_E3 = range(19, 27)
S_IDX, S_W2, S_FORWARD, R_ACROSS = range(19, 23)
MESH = pl.DeviceIdType.MESH
BF16 = jnp.bfloat16
F32 = jnp.float32


def flip(k, offset):
    bit = 1
    while bit <= offset:
        if offset & bit:
            k = k + bit - 2 * bit * ((k // bit) % 2)
        bit *= 2
    return k


def dot(a, b):
    return jnp.dot(a, b, preferred_element_type=F32)


def dot_t(a, b):
    return lax.dot_general(a, b, (((1,), (1,)), ((), ())), preferred_element_type=F32)


def relu_round(x):
    return jnp.maximum(x, 0.0).astype(BF16)


def kernel(
    D,
    R,
    tables,
    indices_h,
    lengths_h,
    dense_h,
    bottom_first_h,
    bottom_second_h,
    bottom_third_h,
    top_first,
    top_second,
    top_third,
    top_fourth,
    top_last_h,
    out,
    indices,
    bag_lengths,
    dense,
    bottom_first,
    bottom_second,
    bottom_third,
    top_last,
    last,
    table_v,
    table_t,
    w1,
    w2,
    w3,
    w4,
    own_idx,
    pair_idx,
    out_idx,
    recv_idx,
    part,
    recv_pool,
    recv_dots,
    bottom,
    first,
    act1,
    third,
    recv_third,
    sem,
):
    B = indices.shape[2]
    rows, E = tables.shape
    X = R // 2
    group = LANES // (2 * B)
    per_table = D // TAB
    me = lax.axis_index("rows")
    k = lax.axis_index("rep")
    core = k % 2
    x = k // 2
    mate = flip(k, 1)
    low, high = D // 2, D
    early = max(D // EARLY, 1)

    barrier = pltpu.get_barrier_semaphore()

    def greet(device):
        pl.semaphore_signal(barrier, inc=1, device_id=device, device_id_type=MESH)

    def local(src, dst, i):
        copy = pltpu.make_async_copy(src, dst, sem.at[i])
        copy.start()
        return copy

    def remote(src, dst, ssem, rsem, device):
        return pltpu.make_async_remote_copy(
            src_ref=src,
            dst_ref=dst,
            send_sem=sem.at[ssem],
            recv_sem=sem.at[rsem],
            device_id=device,
            device_id_type=MESH,
        )

    def send(src, dst, ssem, rsem, device):
        remote(src, dst, ssem, rsem, device).start()

    def arrive(dst, rsem):
        remote(dst, dst, rsem, rsem, (me, mate)).wait_recv()

    def sent(src, ssem):
        remote(src, src, ssem, ssem, (me, mate)).wait_send()

    def sent_blocks(stack, count, ssem):
        while count:
            now = min(count, stack.shape[0])
            sent(stack.at[pl.ds(0, now)], ssem)
            count -= now

    def own_tile():
        lens = bag_lengths[...].reshape(TAB, 1, B)
        slot = lax.broadcasted_iota(jnp.int32, (TAB, HOT, B), 1)
        own_idx[...] = jnp.full(own_idx.shape, -1, jnp.int32)
        own_idx[:, :, :B] = jnp.where(slot < lens, indices[...], -1)
        place = B * (2 * (me % group) + core)
        slot = lax.broadcasted_iota(jnp.int32, (HOT, LANES), 0)
        tiles = []
        for t in range(TAB):
            entry = own_idx[t]
            many = jnp.ones(entry.shape, jnp.int32)
            again = entry < 0
            for r in range(1, HOT):
                other = pltpu.roll(entry, r, 0)
                same = entry == other
                many = many + jnp.where(same, 1, 0)
                again = jnp.logical_or(again, jnp.logical_and(same, slot >= r))
            entry = jnp.where(again, -1, entry + many * SPAN)
            tiles.append(pltpu.roll(entry, place, 1))
        return jnp.stack(tiles)

    deep = w3.shape[1]

    def strip(o):
        return top_third.at[pl.ds(pl.multiple_of(flip(x, o) * deep, deep), deep)]

    def finish():
        total = recv_third[0]
        for n in range(1, X):
            total = total + recv_third[n]
        fourth_in = relu_round(total)
        last_in = relu_round(dot_t(w4[...].reshape(last.shape[0], -1), fourth_in))
        out[...] = jnp.sum(last_in.astype(F32) * last[...], axis=0)

    def last_column():
        row = top_last[...].reshape(1, -1).astype(F32)
        last[...] = jnp.broadcast_to(row, (B, row.shape[1])).T

    for o in range(1, R):
        greet((me, flip(k, o)))
    get_idx = local(indices_h, indices, 0)
    get_len = local(lengths_h, bag_lengths, 1)

    @pl.when(core == 0)
    def follower():
        later = [local(top_fourth, w4.at[k], 2), local(top_last_h, top_last, 3)]
        get_idx.wait()
        get_len.wait()
        pair_idx[...] = own_tile()
        pl.semaphore_wait(barrier, R - 1)
        up = (me, mate)
        send(pair_idx, pair_idx, S_IDX, R_IDX, up)
        send(dense_h, dense.at[k], S_DENSE, R_DENSE, up)
        for o in range(1, X):
            lead = (me, flip(k, 2 * o + 1))
            send(dense_h, dense.at[k], S_DENSE, R_DENSE, lead)
            send(top_first, w1.at[k], S_W1, R_W1, lead)
            send(strip(o), w3.at[k], S_W3, R_W3, lead)
            send(top_fourth, w4.at[k], S_OWN, R_ACROSS + 2 * o, (me, flip(k, 2 * o)))
        send(top_first, w1.at[k], S_W1, R_W1, up)
        send(top_second, w2.at[0], S_W2, R_W2, up)
        send(strip(0), w3.at[k], S_W3, R_W3, up)
        send(top_fourth, w4.at[k], S_OWN, R_DOWN, up)
        if X > 1:
            arrive(w3.at[pl.ds(0, X - 1)], R_W3)
        for o in range(1, X):
            send(w3.at[o - 1], w3.at[mate], S_W3, R_W3, (me, flip(k, 2 * o + 1)))
        arrive(w4.at[mate], R_ACROSS)
        for o in range(1, X):
            send(w4.at[mate], w4.at[mate], S_FORWARD, R_ACROSS + 2 * o + 1, (me, flip(k, 2 * o)))
        for h in range(2):
            for o in range(1, X):
                block = w4.at[flip(k, 2 * o + h)]
                arrive(block, R_ACROSS + 2 * o + h)
                send(block, block, S_FORWARD, R_DOWN, up)
        for copy in later:
            copy.wait()
        last_column()
        arrive(recv_third, R_E4)
        finish()
        sent(pair_idx, S_IDX)
        sent(w2.at[0], S_W2)
        sent_blocks(dense, X, S_DENSE)
        sent_blocks(w1, X, S_W1)
        sent_blocks(w3, 2 * X - 1, S_W3)
        sent_blocks(w4, X, S_OWN)
        sent_blocks(w4, 3 * (X - 1), S_FORWARD)

    @pl.when(core == 1)
    def leader():
        for d in range(1, D):
            greet((flip(me, d), k))
        get_dense = local(dense_h, dense.at[k], 2)
        get_bottom = [
            local(bottom_first_h, bottom_first, 3),
            local(bottom_second_h, bottom_second, 4),
            local(bottom_third_h, bottom_third, 5),
        ]
        get_table = local(tables, table_v, 6)
        get_idx.wait()
        get_len.wait()
        later = [local(top_second, w2.at[1], 0), local(top_first, w1.at[k], 1)]
        mine = own_tile()
        pl.semaphore_wait(barrier, D - 1 + R - 1)
        arrive(pair_idx, R_IDX)
        out_idx[:, :HOT, :] = jnp.maximum(mine, pair_idx[...])

        for d in reversed(range(1, D)):
            peer = flip(me, d)
            send(
                out_idx.at[peer // per_table],
                recv_idx.at[me],
                S_E1,
                R_E1A if d < low else R_E1B,
                (peer, k),
            )
        recv_idx[me] = out_idx[me // per_table]
        for o in range(1, X):
            lead = (me, flip(k, 2 * o))
            send(dense_h, dense.at[k], S_DENSE, R_DENSE, lead)
            send(top_first, w1.at[k], S_W1, R_W1, lead)
            send(strip(o), w3.at[o - 1], S_W3, R_W3, (me, mate))
        send(top_fourth, w4.at[k], S_OWN, R_ACROSS, (me, mate))

        get_table.wait()
        table_t[...] = table_v[...].T

        offset = (me % per_table) * rows
        sub = lax.broadcasted_iota(jnp.int32, (PACK, LANES), 0)
        zero = jnp.zeros((PACK, LANES), BF16)

        def lookup(g):
            base = group * g
            entry = recv_idx[base, :HOT, :]
            for i in range(1, group):
                entry = jnp.maximum(entry, recv_idx[base + i, :HOT, :])
            codes, counts = [], []
            for s in range(HOT):
                row = jnp.broadcast_to(entry[s : s + 1, :], (PACK, LANES))
                spot = (row & (SPAN - 1)) - offset
                hit = jnp.logical_and((spot & (PACK - 1)) == sub, row >= 0)
                codes.append(jnp.where(hit, spot >> SHIFT, -1).astype(F32).astype(BF16))
                counts.append((row // SPAN).astype(F32).astype(BF16))
            partial = jnp.zeros((E, LANES), F32)
            for c in range(rows // CHUNK):
                chunk = []
                for n in range(c * CHUNK // PACK, (c + 1) * CHUNK // PACK):
                    total = zero
                    for code, count in zip(codes, counts):
                        total = jnp.where(code == jnp.asarray(n, BF16), count, total)
                    chunk.append(total)
                partial = partial + dot(
                    table_t[:, c * CHUNK : (c + 1) * CHUNK], jnp.concatenate(chunk, axis=0)
                )
            part[pl.ds(base, group)] = partial.T.reshape(group, 2 * B, E)

        def run(base, count):
            if count == group:
                lookup(base // group)
            else:
                pl.loop(0, count // group)(lambda g: lookup(base // group + g))

        def back(peer, to, rsem):
            send(part.at[peer], recv_pool.at[x * D + me], S_E2, rsem, (peer, to))

        def second_send(d):
            peer = flip(me, d)

            @pl.when(peer < early)
            def crossing():
                for o in range(1, X):
                    back(peer, flip(k, 2 * o), R_E2X)

            if d:

                @pl.when(peer >= early)
                def straight():
                    back(peer, k, R_E2)

        def second_send_late(d):
            peer = flip(me, d)

            @pl.when(peer < early)
            def straight():
                back(peer, k, R_E2)

        arrive(recv_idx.at[pl.ds(0, low - 1)], R_E1A)
        run(me // low * low, low)
        for d in reversed(range(low)):
            second_send(d)
        arrive(recv_idx.at[pl.ds(0, low)], R_E1B)
        run((1 - me // low) * low, low)
        for d in reversed(range(low, high)):
            second_send(d)
        recv_pool[x * D + me] = part[me]
        get_dense.wait()
        for copy in get_bottom:
            copy.wait()
        later += [
            local(strip(0), w3.at[k], 2),
            local(top_fourth, w4.at[k], 3),
            local(top_last_h, top_last, 4),
        ]
        arrive(dense.at[pl.ds(0, R - 1)], R_DENSE)
        arrive(w1.at[pl.ds(0, R - 1)], R_W1)
        lower = relu_round(dot(dense[...].reshape(R * B, -1), bottom_first[...]))
        middle = relu_round(dot(lower, bottom_second[...]))
        bottom_out = jnp.maximum(dot(middle, bottom_third[...]), 0.0)
        for d in reversed(range(1, D)):
            second_send_late(d)
        for copy in later:
            copy.wait()
        last_column()
        bottom[...] = bottom_out.reshape(X, 2 * B, E)
        bottom_in = bottom_out.astype(BF16)
        n1, n2 = w1.shape[2], w2.shape[2]
        for n in range(R):
            first[:, :, n * n1 : (n + 1) * n1] = dot(bottom_in, w1[n, :E, :]).reshape(
                X, 2 * B, n1
            )
        n3 = w3.shape[2]
        lane = lax.broadcasted_iota(jnp.int32, (2 * B, E), 1)

        def interact(y):
            features = [bottom[y]]
            for t in range(TAB):
                pooled = recv_pool[y * D + t * per_table]
                for i in range(1, per_table):
                    pooled = pooled + recv_pool[y * D + t * per_table + i]
                features.append(pooled)
            dots = jnp.zeros((2 * B, E), F32)
            p = 0
            for i in range(TAB + 1):
                for j in range(i + 1, TAB + 1):
                    value = jnp.sum(features[i] * features[j], axis=1, keepdims=True)
                    dots = jnp.where(lane == p, value, dots)
                    p += 1
            recv_dots[y] = dots.astype(BF16)

        def top(y):
            dots = recv_dots[y][:, : TAB * (TAB + 1) // 2]
            for n in range(R):
                act1[:, n * n1 : (n + 1) * n1] = relu_round(
                    first[y, :, n * n1 : (n + 1) * n1] + dot(dots, w1[n, E:, :])
                )
            act2 = jnp.concatenate([relu_round(dot(act1[...], w2[j])) for j in range(2)], axis=1)
            for n in range(R):
                third[pl.ds(2 * y, 2), :, n * n3 : (n + 1) * n3] = dot(act2, w3[n]).reshape(
                    2, B, n3
                )

        def weights():
            arrive(w2.at[0], R_W2)
            arrive(w3.at[pl.ds(0, R - 1)], R_W3)

        def others():
            for o in range(1, X):
                top(flip(x, o))
                for h in range(2):
                    to = flip(k, 2 * o + 1 - h)
                    send(third.at[to], recv_third.at[x], S_E4, R_E4, (me, to))

        def own():
            top(x)
            send(third.at[mate], recv_third.at[x], S_E4, R_E4, (me, mate))
            recv_third[x] = third[k]

        @pl.when(me < early)
        def ahead():
            if X > 1:
                arrive(recv_pool.at[pl.ds(0, (X - 1) * D)], R_E2X)
            for o in range(1, X):
                interact(flip(x, o))
            weights()
            others()
            arrive(recv_pool.at[pl.ds(0, D - 1)], R_E2)
            interact(x)
            own()

        @pl.when(me >= early)
        def behind():
            arrive(recv_pool.at[pl.ds(0, D - 1)], R_E2)
            interact(x)
            for o in range(1, X):
                send(recv_dots.at[x], recv_dots.at[x], S_E3, R_E3, (me, flip(k, 2 * o)))
            weights()
            own()
            if X > 1:
                arrive(recv_dots.at[pl.ds(0, X - 1)], R_E3)
            others()

        arrive(w4.at[pl.ds(0, R - 1)], R_DOWN)
        if X > 1:
            arrive(recv_third.at[pl.ds(0, X - 1)], R_E4)
        finish()
        sent(recv_idx.at[pl.ds(0, D - 1)], S_E1)
        sent_blocks(recv_pool, D - 1 + early * (X - 1), S_E2)
        sent(w4.at[k], S_OWN)
        sent(third.at[pl.ds(0, R - 1)], S_E4)
        if X > 1:
            sent_blocks(dense, X - 1, S_DENSE)
            sent_blocks(w1, X - 1, S_W1)
            sent_blocks(w3, X - 1, S_W3)

            @pl.when(me >= early)
            def sent_dots():
                sent(recv_dots.at[pl.ds(0, X - 1)], S_E3)


def body(*args):
    (tables, indices, bag_lengths, dense, b1, b2, b3, t1, t2, t3, t4, last) = args
    D = lax.axis_size("rows")
    R = lax.axis_size("rep")
    B = indices.shape[0]
    indices = jnp.transpose(indices, (1, 2, 0))
    bag_lengths = jnp.transpose(bag_lengths)
    t4 = jnp.transpose(t4)
    rows, E = tables.shape
    X = R // 2
    hbm = pl.BlockSpec(memory_space=pl.ANY)
    tile = pltpu.VMEM((TAB, HOT, LANES), jnp.int32)
    result = pl.pallas_call(
        functools.partial(kernel, D, R),
        out_shape=pltpu.VMEM((B,), F32),
        in_specs=[hbm] * 12,
        out_specs=pl.BlockSpec(memory_space=pltpu.VMEM),
        scratch_shapes=[
            pltpu.VMEM(indices.shape, jnp.int32),
            pltpu.VMEM(bag_lengths.shape, jnp.int32),
            pltpu.VMEM((R,) + dense.shape, BF16),
            pltpu.VMEM(b1.shape, BF16),
            pltpu.VMEM(b2.shape, BF16),
            pltpu.VMEM(b3.shape, BF16),
            pltpu.VMEM(last.shape, BF16),
            pltpu.VMEM((last.shape[0], B), F32),
            pltpu.VMEM((rows, E), BF16),
            pltpu.VMEM((E, rows), BF16),
            pltpu.VMEM((R,) + t1.shape, BF16),
            pltpu.VMEM((2,) + t2.shape, BF16),
            pltpu.VMEM((R, 2 * t2.shape[1], t3.shape[1]), BF16),
            pltpu.VMEM((R,) + t4.shape, BF16),
            tile,
            tile,
            pltpu.VMEM((TAB, HOT, LANES), jnp.int32),
            pltpu.VMEM((D, HOT, LANES), jnp.int32),
            pltpu.VMEM((D, 2 * B, E), F32),
            pltpu.VMEM((X * D, 2 * B, E), F32),
            pltpu.VMEM((X, 2 * B, E), BF16),
            pltpu.VMEM((X, 2 * B, E), F32),
            pltpu.VMEM((X, 2 * B, R * t1.shape[1]), F32),
            pltpu.VMEM((2 * B, R * t1.shape[1]), BF16),
            pltpu.VMEM((R, B, R * t3.shape[1]), F32),
            pltpu.VMEM((X, B, R * t3.shape[1]), F32),
            pltpu.SemaphoreType.DMA((max(27, R_ACROSS + R),)),
        ],
        compiler_params=pltpu.CompilerParams(collective_id=0, has_side_effects=True),
    )(tables, indices, bag_lengths, dense, b1, b2, b3, t1, t2, t3, t4, last)
    return result


def solution(mesh):
    placed = (
        P("rows", None),
        P(("rows", "rep"), None, None),
        P(("rows", "rep"), None),
        P(("rows", "rep"), None),
        P(),
        P(),
        P(),
        P(None, "rep"),
        P(None, "rep"),
        P(None, "rep"),
        P(None, "rep"),
        P(),
    )
    return jax.shard_map(
        body, mesh=mesh, in_specs=placed, out_specs=P(("rows", "rep")), check_vma=False
    )
```

time: 19.8 us -> 18.2 us (0.919)
  Pallas kernels: 19.1 us -> 17.5 us
    pallas_call x1, Pallas kernels: 19.1 us -> 17.5 us  [body(): pl.pallas_call(functools.partial(kernel, D, R), out_shape=pltpu.VMEM((B,)...]
where the time goes in v3:
time: 18.2 us; the launch traced here: 18 us
  Pallas kernels  17.5 us (96%)
  local copies, waits for them, and re-layouts  0.51 us (3%)
    pallas_call x1, Pallas kernels, body(): pl.pallas_call(functools.partial(kernel, D, R), out_shape=pltpu.VMEM((B,)...  17.5 us
    unnamed x1, local copies, waits for them, and re-layouts  0.51 us

profile of v3, /device:TPU:0, one launch (start us, length us, event | category | flops | bytes accessed | tf_op | source)
XLA Modules:
  0.0 18.0 jit_solution(10827824490437509324)
XLA Ops:
  0.0 17.5 %shard_map.118 = f32[16]{0:T(128)S(1)} custom-call(bf16[2048,128]{1,0:T(8,128)(2,1)} %tables.1, s32[8,8,16]{2,1,0:T(8,128)} %bitcast.4, s32[8,16]{1,0:T(8,128)} %bitcast.5, bf16[16,13]{1,0:T(8,128)(2,1)} %dense_h.1, bf16[13,512]{1,0:T(8,128)(2,1)} %bottom_first_h.1, bf16[512,256]{1,0:T(8,128)(2,1)} %bottom_second_h.1, bf16[256,128]{1,0:T(8,128)(2,1)} %bottom_third_h.1, ...), custom_call_target="tpu_custom_call" | custom-call | tf_op jit(solution)/shard_map/pallas_call | solution.py:460
  17.5 0.5 %copy.14 = f32[16]{0:T(128)} copy(f32[16]{0:T(128)S(1)} %shard_map.118) | data formatting | bytes 128

commit v4 on v3

--- a/solution.py
+++ b/solution.py
@@ -13,10 +13,10 @@
 PACK = 16
 SHIFT = 4
 CHUNK = 256
-EARLY = 4
+EARLY = 8
 SPAN = 65536
 S_DENSE, S_W1, S_W3, S_OWN, S_E4, R_IDX, R_DENSE, R_W1, R_W2, R_W3, R_E4, R_DOWN = range(7, 19)
-S_E1, S_E2, S_E3, R_E1A, R_E1B, R_E2, R_E2X, R_E3 = range(19, 27)
+S_E1, S_E2, S_E3, R_E1, R_E1_LATE, R_E2, R_E2X, R_E3 = range(19, 27)
 S_IDX, S_W2, S_FORWARD, R_ACROSS = range(19, 23)
 MESH = pl.DeviceIdType.MESH
 BF16 = jnp.bfloat16
@@ -249,7 +249,7 @@
                 out_idx.at[peer // per_table],
                 recv_idx.at[me],
                 S_E1,
-                R_E1A if d < low else R_E1B,
+                R_E1 + me // low,
                 (peer, k),
             )
         recv_idx[me] = out_idx[me // per_table]
@@ -301,35 +301,31 @@
         def back(peer, to, rsem):
             send(part.at[peer], recv_pool.at[x * D + me], S_E2, rsem, (peer, to))
 
-        def second_send(d):
-            peer = flip(me, d)
-
-            @pl.when(peer < early)
-            def crossing():
+        def second_send(r):
+            if r < early:
                 for o in range(1, X):
-                    back(peer, flip(k, 2 * o), R_E2X)
-
-            if d:
-
-                @pl.when(peer >= early)
-                def straight():
-                    back(peer, k, R_E2)
-
-        def second_send_late(d):
-            peer = flip(me, d)
-
-            @pl.when(peer < early)
+                    back(r, flip(k, 2 * o), R_E2X)
+            else:
+                second_send_straight(r)
+
+        def second_send_straight(r):
+            @pl.when(me != r)
             def straight():
-                back(peer, k, R_E2)
-
-        arrive(recv_idx.at[pl.ds(0, low - 1)], R_E1A)
-        run(me // low * low, low)
-        for d in reversed(range(low)):
-            second_send(d)
-        arrive(recv_idx.at[pl.ds(0, low)], R_E1B)
-        run((1 - me // low) * low, low)
-        for d in reversed(range(low, high)):
-            second_send(d)
+                back(r, k, R_E2)
+
+        for half in range(2):
+
+            @pl.when(me // low == half)
+            def from_own_half():
+                arrive(recv_idx.at[pl.ds(0, low - 1)], R_E1 + half)
+
+            @pl.when(me // low != half)
+            def from_other_half():
+                arrive(recv_idx.at[pl.ds(0, low)], R_E1 + half)
+
+            run(half * low, low)
+            for r in range(half * low, (half + 1) * low):
+                second_send(r)
         recv_pool[x * D + me] = part[me]
         get_dense.wait()
         for copy in get_bottom:
@@ -344,8 +340,8 @@
         lower = relu_round(dot(dense[...].reshape(R * B, -1), bottom_first[...]))
         middle = relu_round(dot(lower, bottom_second[...]))
         bottom_out = jnp.maximum(dot(middle, bottom_third[...]), 0.0)
-        for d in reversed(range(1, D)):
-            second_send_late(d)
+        for r in range(early):
+            second_send_straight(r)
         for copy in later:
             copy.wait()
         last_column()

time: 18.2 us -> 17.2 us (0.945)
  Pallas kernels: 17.5 us -> 16.5 us
    pallas_call x1, Pallas kernels: 17.5 us -> 16.5 us  [body(): pl.pallas_call(functools.partial(kernel, D, R), out_shape=pltpu.VMEM((B,)...]
where the time goes in v4:
time: 17.2 us; the launch traced here: 17 us
  Pallas kernels  16.5 us (96%)
  local copies, waits for them, and re-layouts  0.51 us (3%)
    pallas_call x1, Pallas kernels, body(): pl.pallas_call(functools.partial(kernel, D, R), out_shape=pltpu.VMEM((B,)...  16.5 us
    unnamed x1, local copies, waits for them, and re-layouts  0.51 us

profile of v4, /device:TPU:0, one launch (start us, length us, event | category | flops | bytes accessed | tf_op | source)
XLA Modules:
  0.0 17.0 jit_solution(11575650864378967734)
XLA Ops:
  0.0 16.5 %shard_map.118 = f32[16]{0:T(128)S(1)} custom-call(bf16[2048,128]{1,0:T(8,128)(2,1)} %tables.1, s32[8,8,16]{2,1,0:T(8,128)} %bitcast.4, s32[8,16]{1,0:T(8,128)} %bitcast.5, bf16[16,13]{1,0:T(8,128)(2,1)} %dense_h.1, bf16[13,512]{1,0:T(8,128)(2,1)} %bottom_first_h.1, bf16[512,256]{1,0:T(8,128)(2,1)} %bottom_second_h.1, bf16[256,128]{1,0:T(8,128)(2,1)} %bottom_third_h.1, ...), custom_call_target="tpu_custom_call" | custom-call | tf_op jit(solution)/shard_map/pallas_call | solution.py:456
  16.5 0.5 %copy.14 = f32[16]{0:T(128)} copy(f32[16]{0:T(128)S(1)} %shard_map.118) | data formatting | bytes 128

commit v5 on v4

--- a/solution.py
+++ b/solution.py
@@ -12,11 +12,11 @@
 LANES = 128
 PACK = 16
 SHIFT = 4
-CHUNK = 256
+CHUNK = 512
 EARLY = 8
 SPAN = 65536
 S_DENSE, S_W1, S_W3, S_OWN, S_E4, R_IDX, R_DENSE, R_W1, R_W2, R_W3, R_E4, R_DOWN = range(7, 19)
-S_E1, S_E2, S_E3, R_E1, R_E1_LATE, R_E2, R_E2X, R_E3 = range(19, 27)
+S_E1, S_E2, S_E3, R_E1, R_E1_LATE, R_E2, R_E2X, R_E2Y, R_E3 = range(19, 28)
 S_IDX, S_W2, S_FORWARD, R_ACROSS = range(19, 23)
 MESH = pl.DeviceIdType.MESH
 BF16 = jnp.bfloat16
@@ -304,7 +304,12 @@
         def second_send(r):
             if r < early:
                 for o in range(1, X):
-                    back(r, flip(k, 2 * o), R_E2X)
+                    back(r, flip(k, 2 * o), R_E2X + (R_E2Y - R_E2X) * (me // low))
+
+                @pl.when(x == 0)
+                def at_once():
+                    second_send_straight(r)
+
             else:
                 second_send_straight(r)
 
@@ -340,8 +345,11 @@
         lower = relu_round(dot(dense[...].reshape(R * B, -1), bottom_first[...]))
         middle = relu_round(dot(lower, bottom_second[...]))
         bottom_out = jnp.maximum(dot(middle, bottom_third[...]), 0.0)
-        for r in range(early):
-            second_send_straight(r)
+        @pl.when(x > 0)
+        def not_urgent():
+            for r in range(early):
+                second_send_straight(r)
+
         for copy in later:
             copy.wait()
         last_column()
@@ -355,20 +363,34 @@
         n3 = w3.shape[2]
         lane = lax.broadcasted_iota(jnp.int32, (2 * B, E), 1)
 
-        def interact(y):
-            features = [bottom[y]]
-            for t in range(TAB):
-                pooled = recv_pool[y * D + t * per_table]
-                for i in range(1, per_table):
-                    pooled = pooled + recv_pool[y * D + t * per_table + i]
-                features.append(pooled)
-            dots = jnp.zeros((2 * B, E), F32)
+        def feature(y, t):
+            pooled = recv_pool[y * D + t * per_table]
+            for i in range(1, per_table):
+                pooled = pooled + recv_pool[y * D + t * per_table + i]
+            return pooled
+
+        def pairs(y, features, dots, wanted):
             p = 0
             for i in range(TAB + 1):
                 for j in range(i + 1, TAB + 1):
-                    value = jnp.sum(features[i] * features[j], axis=1, keepdims=True)
-                    dots = jnp.where(lane == p, value, dots)
+                    if wanted(j):
+                        value = jnp.sum(features[i] * features[j], axis=1, keepdims=True)
+                        dots = jnp.where(lane == p, value, dots)
                     p += 1
+            return dots
+
+        def interact(y, between=None):
+            dots = jnp.zeros((2 * B, E), F32)
+            features = [bottom[y]]
+            if between is None:
+                features += [feature(y, t) for t in range(TAB)]
+                dots = pairs(y, features, dots, lambda j: True)
+            else:
+                features += [feature(y, t) for t in range(TAB // 2)]
+                dots = pairs(y, features, dots, lambda j: j <= TAB // 2)
+                between()
+                features += [feature(y, t) for t in range(TAB // 2, TAB)]
+                dots = pairs(y, features, dots, lambda j: j > TAB // 2)
             recv_dots[y] = dots.astype(BF16)
 
         def top(y):
@@ -399,12 +421,34 @@
             send(third.at[mate], recv_third.at[x], S_E4, R_E4, (me, mate))
             recv_third[x] = third[k]
 
-        @pl.when(me < early)
+        @pl.when(jnp.logical_and(me < early, x == 0))
+        def foremost():
+            arrive(recv_pool.at[pl.ds(0, D - 1)], R_E2)
+            interact(x)
+            weights()
+            own()
+            if X > 1:
+                lower = pl.ds(0, (X - 1) * low)
+                arrive(recv_pool.at[lower], R_E2X)
+                if X == 2:
+                    interact(flip(x, 1), lambda: arrive(recv_pool.at[lower], R_E2Y))
+                else:
+                    arrive(recv_pool.at[lower], R_E2Y)
+                    for o in range(1, X):
+                        interact(flip(x, o))
+            others()
+
+        @pl.when(jnp.logical_and(me < early, x > 0))
         def ahead():
             if X > 1:
-                arrive(recv_pool.at[pl.ds(0, (X - 1) * D)], R_E2X)
-            for o in range(1, X):
-                interact(flip(x, o))
+                lower = pl.ds(0, (X - 1) * low)
+                arrive(recv_pool.at[lower], R_E2X)
+                if X == 2:
+                    interact(flip(x, 1), lambda: arrive(recv_pool.at[lower], R_E2Y))
+                else:
+                    arrive(recv_pool.at[lower], R_E2Y)
+                    for o in range(1, X):
+                        interact(flip(x, o))
             weights()
             others()
             arrive(recv_pool.at[pl.ds(0, D - 1)], R_E2)
@@ -485,7 +529,7 @@
             pltpu.VMEM((2 * B, R * t1.shape[1]), BF16),
             pltpu.VMEM((R, B, R * t3.shape[1]), F32),
             pltpu.VMEM((X, B, R * t3.shape[1]), F32),
-            pltpu.SemaphoreType.DMA((max(27, R_ACROSS + R),)),
+            pltpu.SemaphoreType.DMA((max(28, R_ACROSS + R),)),
         ],
         compiler_params=pltpu.CompilerParams(collective_id=0, has_side_effects=True),
     )(tables, indices, bag_lengths, dense, b1, b2, b3, t1, t2, t3, t4, last)

time: 17.2 us -> 17.1 us (level)
  no operation moved by 1% of the time
where the time goes in v5:
time: 17.1 us; the launch traced here: 17 us
  Pallas kernels  16.5 us (96%)
  local copies, waits for them, and re-layouts  0.51 us (3%)
    pallas_call x1, Pallas kernels, body(): pl.pallas_call(functools.partial(kernel, D, R), out_shape=pltpu.VMEM((B,)...  16.5 us
    unnamed x1, local copies, waits for them, and re-layouts  0.51 us

profile of v5, /device:TPU:0, one launch (start us, length us, event | category | flops | bytes accessed | tf_op | source)
XLA Modules:
  0.0 17.0 jit_solution(13256744561669573451)
XLA Ops:
  0.0 16.5 %shard_map.118 = f32[16]{0:T(128)S(1)} custom-call(bf16[2048,128]{1,0:T(8,128)(2,1)} %tables.1, s32[8,8,16]{2,1,0:T(8,128)} %bitcast.4, s32[8,16]{1,0:T(8,128)} %bitcast.5, bf16[16,13]{1,0:T(8,128)(2,1)} %dense_h.1, bf16[13,512]{1,0:T(8,128)(2,1)} %bottom_first_h.1, bf16[512,256]{1,0:T(8,128)(2,1)} %bottom_second_h.1, bf16[256,128]{1,0:T(8,128)(2,1)} %bottom_third_h.1, ...), custom_call_target="tpu_custom_call" | custom-call | tf_op jit(solution)/shard_map/pallas_call | solution.py:500
  16.5 0.5 %copy.14 = f32[16]{0:T(128)} copy(f32[16]{0:T(128)S(1)} %shard_map.118) | data formatting | bytes 128

commit v6 on v4

--- a/solution.py
+++ b/solution.py
@@ -12,7 +12,7 @@
 LANES = 128
 PACK = 16
 SHIFT = 4
-CHUNK = 256
+CHUNK = 512
 EARLY = 8
 SPAN = 65536
 S_DENSE, S_W1, S_W3, S_OWN, S_E4, R_IDX, R_DENSE, R_W1, R_W2, R_W3, R_E4, R_DOWN = range(7, 19)
@@ -279,7 +279,7 @@
                 hit = jnp.logical_and((spot & (PACK - 1)) == sub, row >= 0)
                 codes.append(jnp.where(hit, spot >> SHIFT, -1).astype(F32).astype(BF16))
                 counts.append((row // SPAN).astype(F32).astype(BF16))
-            partial = jnp.zeros((E, LANES), F32)
+            partial = jnp.zeros((LANES, E), F32)
             for c in range(rows // CHUNK):
                 chunk = []
                 for n in range(c * CHUNK // PACK, (c + 1) * CHUNK // PACK):
@@ -287,10 +287,13 @@
                     for code, count in zip(codes, counts):
                         total = jnp.where(code == jnp.asarray(n, BF16), count, total)
                     chunk.append(total)
-                partial = partial + dot(
-                    table_t[:, c * CHUNK : (c + 1) * CHUNK], jnp.concatenate(chunk, axis=0)
+                partial = partial + lax.dot_general(
+                    jnp.concatenate(chunk, axis=0),
+                    table_v[c * CHUNK : (c + 1) * CHUNK, :],
+                    (((0,), (0,)), ((), ())),
+                    preferred_element_type=F32,
                 )
-            part[pl.ds(base, group)] = partial.T.reshape(group, 2 * B, E)
+            part[pl.ds(base, group)] = partial.reshape(group, 2 * B, E)
 
         def run(base, count):
             if count == group:

time: 17.2 us -> 17.2 us (level)
  no operation moved by 1% of the time
where the time goes in v6:
time: 17.2 us; the launch traced here: 17 us
  Pallas kernels  16.5 us (96%)
  local copies, waits for them, and re-layouts  0.51 us (3%)
    pallas_call x1, Pallas kernels, body(): pl.pallas_call(functools.partial(kernel, D, R), out_shape=pltpu.VMEM((B,)...  16.5 us
    unnamed x1, local copies, waits for them, and re-layouts  0.51 us

profile of v6, /device:TPU:0, one launch (start us, length us, event | category | flops | bytes accessed | tf_op | source)
XLA Modules:
  0.0 17.0 jit_solution(4428775581632115146)
XLA Ops:
  0.0 16.5 %shard_map.118 = f32[16]{0:T(128)S(1)} custom-call(bf16[2048,128]{1,0:T(8,128)(2,1)} %tables.1, s32[8,8,16]{2,1,0:T(8,128)} %bitcast.4, s32[8,16]{1,0:T(8,128)} %bitcast.5, bf16[16,13]{1,0:T(8,128)(2,1)} %dense_h.1, bf16[13,512]{1,0:T(8,128)(2,1)} %bottom_first_h.1, bf16[512,256]{1,0:T(8,128)(2,1)} %bottom_second_h.1, bf16[256,128]{1,0:T(8,128)(2,1)} %bottom_third_h.1, ...), custom_call_target="tpu_custom_call" | custom-call | tf_op jit(solution)/shard_map/pallas_call | solution.py:459
  16.5 0.5 %copy.14 = f32[16]{0:T(128)} copy(f32[16]{0:T(128)S(1)} %shard_map.118) | data formatting | bytes 128
